TPU v7x, 32 devices: a whole 2x2x4 slice. The times are simulated.
32 devices in a mesh: replica: 4 (over y, core), shard: 8 (over z, x).
Axes of the slice: x: 2, y: 2, z: 4, core: 2. Of those that a mesh axis runs over, the one named last changes fastest.
Arguments:
- inputs: bfloat16 [512, 2048], P('replica'), may hold values from -6 to 6
- gate_pre: bfloat16 [512, 8192], P('replica', 'shard'), may hold values from -8 to 8
- up_pre: bfloat16 [512, 8192], P('replica', 'shard'), may hold values from -6 to 6
- hidden_grad: bfloat16 [512, 8192], P('replica', 'shard'), may hold values from -6 to 6
- segment_ids: int32 [4, 128], P('replica'), may hold values from 0 to 15, never falling along the last dimension, each value on 1 to 32 neighbouring positions
- doc_weight: int32 [4, 16], P('replica'), may hold values from 1 to 12
- w_gate: bfloat16 [2048, 8192], P(None, 'shard'), may hold values from -0.0625 to 0.0625
- master: float32 [2048, 8192], P('replica', 'shard'), may hold values from -6 to 6
- moment: float32 [2048, 8192], P('replica', 'shard'), may hold values from -10 to 10
- second: float32 [2048, 8192], P('replica', 'shard'), may hold values from 0.5 to 20
Outputs:
- input_grad: bfloat16 [512, 2048], P(('replica', 'shard'))
- up_grad: bfloat16 [512, 8192], P('replica', 'shard')
- master_new: float32 [2048, 8192], P('replica', 'shard')
- moment_new: float32 [2048, 8192], P('replica', 'shard')
- second_new: float32 [2048, 8192], P('replica', 'shard')
Inputs may be any that keep to these rules, and one draw needn't show every extreme that they name: `segment_ids`: within each group the documents occupy runs of positions numbered 0 to 15 in order, each at most 32 long.
All inputs are finite; a program needn't handle non-finite values.
Results may differ from a plain program's by a relative error of at most 0.0049.
Values sent between devices are 32-bit elements; how exact they have to be, the bound alone decides.
A program may use at most 64 MiB of HBM per device.

v0:
```python
import functools

import jax
import jax.numpy as jnp
from jax import lax
from jax.experimental import pallas as pl
from jax.experimental.pallas import tpu as pltpu
from jax.sharding import PartitionSpec as P

MESH = pl.DeviceIdType.MESH
QUARTERS = 4


def token_weights(segment_ids, doc_weight):
    labels = jnp.arange(doc_weight.shape[1], dtype=jnp.int32)
    onehot = segment_ids[:, :, None] == labels[None, None, :]
    return jnp.sum(jnp.where(onehot, doc_weight[:, None, :], 0), axis=2)


def adamw(grad, master, moment, second):
    moment_new = 0.9 * moment + 0.1 * grad
    second_new = 0.95 * second + 0.05 * grad * grad
    first_fix = moment_new / (1.0 - 0.9**8)
    second_fix = second_new / (1.0 - 0.95**8)
    master_new = master - 0.003 * (first_fix / (jnp.sqrt(second_fix) + 1e-08) + 0.1 * master)
    return master_new, moment_new, second_new


def reduce_path(
    inputs, gate_pre, up_pre, hidden_grad, segment_ids, doc_weight, w_gate, master, moment, second
):
    group_rows = inputs.shape[0]
    replicas = lax.axis_size("replica")
    weights = token_weights(segment_ids, doc_weight)[0]
    local_count = jnp.sum(weights)
    gate_f = gate_pre.astype(jnp.float32)
    sigmoid_gate = jax.nn.sigmoid(gate_f)
    weighted = hidden_grad.astype(jnp.float32) * weights.astype(jnp.float32)[:, None]
    gate_raw = (
        weighted * up_pre.astype(jnp.float32) * sigmoid_gate * (1.0 + gate_f * (1.0 - sigmoid_gate))
    ).astype(jnp.bfloat16)
    up_part = weighted * gate_f * sigmoid_gate
    input_part = lax.dot_general(
        gate_raw, w_gate, (((1,), (1,)), ((), ())), preferred_element_type=jnp.float32
    )
    input_summed = lax.psum_scatter(input_part, "shard", scatter_dimension=0, tiled=True)
    total = lax.psum(local_count, "replica").astype(jnp.float32)
    summed_grad = lax.psum_scatter(
        lax.dot_general(
            inputs, gate_raw, (((0,), (0,)), ((), ())), preferred_element_type=jnp.float32
        ),
        "replica",
        scatter_dimension=0,
        tiled=True,
    )
    scale = jnp.float32(group_rows * replicas) / total
    group_scale = jnp.float32(group_rows) / total
    input_grad = (input_summed * scale).astype(jnp.bfloat16)
    up_grad = (up_part * scale).astype(jnp.bfloat16)
    return (input_grad, up_grad) + adamw(summed_grad * group_scale, master, moment, second)


def flip(index, bit):
    return index + bit - 2 * bit * lax.rem(lax.div(index, bit), 2)


def exchange_kernel(
    x_hbm, gate_hbm, up_hbm, hid_hbm, seg_hbm, dw_hbm, w_hbm,
    xo_hbm, go_hbm, sum_hbm, upo_hbm, gs_hbm,
    xo_ref, go_ref, sum_ref, upo_ref, gs_ref, x_v, gate_v, up_v, hid_v, seg_ref, dw_ref, w_v, x32, g32, part, cnt,
    xp, xq, gr, rs1, rs2, rs3, cntr, lsem, osem, ssem, rsem,
):
    r, s = lax.axis_index("replica"), lax.axis_index("shard")
    replicas = lax.axis_size("replica")
    core, side, across = flip(r, 1), flip(r, 2), flip(flip(r, 1), 2)
    near, mid, far = flip(s, 1), flip(s, 2), flip(s, 4)
    rows, width = x_v.shape[0], xo_ref.shape[1]
    quarter = rows // QUARTERS
    tall = sum_ref.shape[0]
    f32, bf16 = jnp.float32, jnp.bfloat16

    local = []
    for k, (src, dst) in enumerate(
        [
            (x_hbm, x_v), (seg_hbm, seg_ref), (dw_hbm, dw_ref), (gate_hbm, gate_v),
            (hid_hbm, hid_v), (up_hbm, up_v), (w_hbm, w_v),
        ]
    ):
        copy = pltpu.make_async_copy(src, dst, lsem.at[k])
        copy.start()
        local.append(copy)

    barrier = pltpu.get_barrier_semaphore()
    peers = [(core, s), (side, s), (across, s), (r, near), (r, mid), (r, far)]
    for peer in peers:
        pl.semaphore_signal(barrier, inc=1, device_id=peer, device_id_type=MESH)

    started, written = [], []

    def write(src, dst):
        copy = pltpu.make_async_copy(src, dst, osem.at[len(written)])
        copy.start()
        written.append(copy)

    def push(src, dst, peer):
        k = len(started)
        copy = pltpu.make_async_remote_copy(
            src_ref=src, dst_ref=dst, send_sem=ssem.at[k], recv_sem=rsem.at[k],
            device_id=peer, device_id_type=MESH,
        )
        copy.start()
        started.append(copy)
        return copy

    local[0].wait()
    x32[...] = x_v[...].astype(f32)
    own = pl.ds(pl.multiple_of(r * width, width), width)
    xo_ref[pl.ds(0, rows), :] = x_v[:, own]

    local[1].wait()
    local[2].wait()
    docs = dw_ref.shape[1]
    seg = jnp.broadcast_to(seg_ref[...].astype(f32), (128, rows)).T[:, :docs]
    labels = lax.broadcasted_iota(jnp.int32, (rows, docs), 1).astype(f32)
    dw = jnp.broadcast_to(dw_ref[...].astype(f32), (rows, docs))
    tw = jnp.sum(jnp.where(seg == labels, dw, 0.0), axis=1, keepdims=True)
    count = jnp.sum(tw, axis=0, keepdims=True)
    cnt[...] = jnp.broadcast_to(count, cnt.shape)

    pl.semaphore_wait(barrier, len(peers))

    q = lax.rem(s, QUARTERS)

    def at_quarter(index):
        return pl.ds(pl.multiple_of(index * quarter, quarter), quarter)

    def columns(owner):
        return pl.ds(pl.multiple_of(owner * width, width), width)

    x_side = push(x32.at[at_quarter(q), columns(side)], xq.at[0, 0], (side, s))
    x_across = push(x32.at[at_quarter(q), columns(across)], xq.at[1, 0], (across, s))
    x_core = push(x32.at[:, columns(core)], xp, (core, s))
    counts = [push(cnt, cntr.at[k], (peer, s)) for k, peer in enumerate((core, side, across))]

    for k in (3, 4, 5):
        local[k].wait()
    for k in range(QUARTERS):
        at = pl.ds(k * quarter, quarter)
        g = gate_v[at, :].astype(f32)
        sig = jax.nn.sigmoid(g)
        h = hid_v[at, :].astype(f32) * tw[k * quarter : (k + 1) * quarter, :]
        raw = (h * up_v[at, :].astype(f32) * sig * (1.0 + g * (1.0 - sig))).astype(bf16)
        upo_ref[at, :] = h * g * sig
        go_ref[at, :] = raw
        g32[at, :] = raw.astype(f32)

    g_side = [
        push(g32.at[pl.ds(k * quarter, quarter), :], gr.at[1, pl.ds(k * quarter, quarter), :], (side, s))
        for k in range(QUARTERS)
    ]
    g_core = push(g32, gr.at[0], (core, s))

    local[6].wait()
    step = w_v.shape[0] // QUARTERS
    for k in range(QUARTERS):
        part[:, pl.ds(k * step, step)] = lax.dot_general(
            go_ref[pl.ds(0, rows), :], w_v[pl.ds(k * step, step), :],
            (((1,), (1,)), ((), ())), preferred_element_type=f32,
        )

    def block(index):
        return pl.ds(pl.multiple_of(index * tall, tall), tall)

    first = {}
    for slot, (delta, index) in enumerate(
        [(6, flip(flip(near, 2), 4)), (2, flip(near, 2)), (4, flip(near, 4)), (0, near)]
    ):
        first[delta] = (slot, push(part.at[block(index), :], rs1.at[slot], (r, near)))

    def absorb(delta, index):
        slot, copy = first[delta]
        copy.wait_recv()
        part[block(index), :] = part[block(index), :] + rs1[slot]

    def keep_x(group, slot, index):
        xo_ref[pl.ds(pl.multiple_of((group + 2) * rows + index * quarter, quarter), quarter), :] = (
            xq[group, slot].astype(bf16)
        )

    def keep_g(group, k):
        at = pl.ds(k * quarter, quarter)
        go_ref[pl.ds((group + 1) * rows + k * quarter, quarter), :] = gr[group, at, :].astype(bf16)

    def relay_g(k):
        at = pl.ds(k * quarter, quarter)
        g_side[k].wait_recv()
        copy = push(gr.at[1, at, :], gr.at[2, at, :], (core, s))
        keep_g(1, k)
        return copy

    x_near, x_mid = [], []
    for group, copy in enumerate((x_side, x_across)):
        copy.wait_recv()
        x_near.append(push(xq.at[group, 0], xq.at[group, 1], (r, near)))
        x_mid.append(push(xq.at[group, 0], xq.at[group, 2], (r, mid)))
    x_core.wait_recv()
    xo_ref[pl.ds(rows, rows), :] = xp[...].astype(bf16)
    g_core.wait_recv()
    for k in range(QUARTERS):
        keep_g(0, k)
    for group in range(2):
        keep_x(group, 0, q)
    for copy in counts:
        copy.wait_recv()
    total = (cnt[...] + cntr[0] + cntr[1] + cntr[2])[0:1, 0:1]
    scale = f32(rows * replicas) / total
    gs_ref[...] = jnp.broadcast_to(f32(rows) / total, gs_ref.shape)
    upo_ref[...] = upo_ref[...] * scale
    write(xo_ref.at[pl.ds(0, 2 * rows), :], xo_hbm.at[pl.ds(0, 2 * rows), :])
    write(go_ref.at[pl.ds(0, 2 * rows), :], go_hbm.at[pl.ds(0, 2 * rows), :])
    write(gs_ref, gs_hbm)
    write(upo_ref, upo_hbm)

    g_across = [relay_g(0)]
    absorb(6, flip(mid, 4))
    second_far = push(part.at[block(flip(mid, 4)), :], rs2.at[0], (r, mid))
    absorb(2, mid)
    second_own = push(part.at[block(mid), :], rs2.at[1], (r, mid))
    g_across.append(relay_g(1))
    absorb(4, far)
    second_far.wait_recv()
    part[block(far), :] = part[block(far), :] + rs2[0]
    third = push(part.at[block(far), :], rs3, (r, far))
    x_last = []
    for group in range(2):
        x_near[group].wait_recv()
        x_last.append(push(xq.at[group, 1], xq.at[group, 3], (r, mid)))
        keep_x(group, 1, lax.rem(near, QUARTERS))
    g_across.append(relay_g(2))
    for group in range(2):
        x_mid[group].wait_recv()
        keep_x(group, 2, lax.rem(mid, QUARTERS))
    for k in range(2):
        g_across[k].wait_recv()
        keep_g(2, k)
    absorb(0, s)
    second_own.wait_recv()
    g_across.append(relay_g(3))
    for group in range(2):
        x_last[group].wait_recv()
        keep_x(group, 3, lax.rem(flip(near, 2), QUARTERS))
    write(xo_ref.at[pl.ds(2 * rows, 2 * rows), :], xo_hbm.at[pl.ds(2 * rows, 2 * rows), :])
    write(go_ref.at[pl.ds(2 * rows, rows), :], go_hbm.at[pl.ds(2 * rows, rows), :])
    third.wait_recv()
    sum_ref[...] = (part[block(s), :] + rs2[1] + rs3[...]) * scale
    write(sum_ref, sum_hbm)
    for k in range(2, QUARTERS):
        g_across[k].wait_recv()
        keep_g(2, k)
    write(go_ref.at[pl.ds(3 * rows, rows), :], go_hbm.at[pl.ds(3 * rows, rows), :])
    for copy in started:
        copy.wait_send()
    for copy in written:
        copy.wait()


def exchange(inputs, gate_pre, up_pre, hidden_grad, segment_ids, doc_weight, w_gate):
    replicas, shards = lax.axis_size("replica"), lax.axis_size("shard")
    rows, features = inputs.shape
    hidden = gate_pre.shape[1]
    width, tall, quarter = features // replicas, rows // shards, rows // QUARTERS
    f32, bf16 = jnp.float32, jnp.bfloat16
    hbm = pl.BlockSpec(memory_space=pltpu.HBM)
    copies = 30
    return pl.pallas_call(
        exchange_kernel,
        out_shape=(
            jax.ShapeDtypeStruct((replicas * rows, width), bf16),
            jax.ShapeDtypeStruct((replicas * rows, hidden), bf16),
            jax.ShapeDtypeStruct((tall, features), f32),
            jax.ShapeDtypeStruct((rows, hidden), f32),
            jax.ShapeDtypeStruct((8, hidden), f32),
        ),
        in_specs=[hbm] * 7,
        out_specs=(hbm,) * 5,
        scratch_shapes=[
            pltpu.VMEM((replicas * rows, width), bf16),
            pltpu.VMEM((replicas * rows, hidden), bf16),
            pltpu.VMEM((tall, features), f32),
            pltpu.VMEM((rows, hidden), f32),
            pltpu.VMEM((8, hidden), f32),
            pltpu.VMEM((rows, features), bf16),
            pltpu.VMEM((rows, hidden), bf16),
            pltpu.VMEM((rows, hidden), bf16),
            pltpu.VMEM((rows, hidden), bf16),
            pltpu.VMEM(segment_ids.shape, jnp.int32),
            pltpu.VMEM(doc_weight.shape, jnp.int32),
            pltpu.VMEM((features, hidden), bf16),
            pltpu.VMEM((rows, features), f32),
            pltpu.VMEM((rows, hidden), f32),
            pltpu.VMEM((rows, features), f32),
            pltpu.VMEM((8, 128), f32),
            pltpu.VMEM((rows, width), f32),
            pltpu.VMEM((2, QUARTERS, quarter, width), f32),
            pltpu.VMEM((3, rows, hidden), f32),
            pltpu.VMEM((4, tall, features), f32),
            pltpu.VMEM((2, tall, features), f32),
            pltpu.VMEM((tall, features), f32),
            pltpu.VMEM((3, 8, 128), f32),
            pltpu.SemaphoreType.DMA((7,)),
            pltpu.SemaphoreType.DMA((8,)),
            pltpu.SemaphoreType.DMA((copies,)),
            pltpu.SemaphoreType.DMA((copies,)),
        ],
        compiler_params=pltpu.CompilerParams(
            collective_id=0, has_side_effects=True, vmem_limit_bytes=54 * 1024 * 1024
        ),
        cost_estimate=pl.CostEstimate(
            flops=2 * rows * hidden * features, bytes_accessed=40 * 1024 * 1024, transcendentals=0
        ),
        name="exchange",
    )(inputs, gate_pre, up_pre, hidden_grad, segment_ids, doc_weight, w_gate)


def step_kernel(
    x_hbm, g_hbm, sum_hbm, up_hbm, gs_hbm, ma_old, mo_old, se_old,
    ig_hbm, ug_hbm, ma_hbm, mo_hbm, se_hbm,
    x_ref, g_ref, sum_ref, up_ref, gs_ref, ma_ref, mo_ref, se_ref, ig_v, ug_v, ma_v, mo_v, se_v, isem, sems,
):
    band = ma_v.shape[1]
    written, loaded = [], []
    bands = [pl.ds(k * band, band) for k in range(ma_v.shape[0])]
    loads = [(g_hbm, g_ref), (x_hbm, x_ref), (gs_hbm, gs_ref)]
    for at in bands:
        loads += [
            (old.at[at, :], new.at[at, :])
            for old, new in ((mo_old, mo_ref), (se_old, se_ref), (ma_old, ma_ref))
        ]
    for k, (src, dst) in enumerate(loads + [(sum_hbm, sum_ref), (up_hbm, up_ref)]):
        copy = pltpu.make_async_copy(src, dst, isem.at[k])
        copy.start()
        loaded.append(copy)

    def write(src, dst):
        copy = pltpu.make_async_copy(src, dst, sems.at[len(written)])
        copy.start()
        written.append(copy)

    for copy in loaded[:3]:
        copy.wait()
    group_scale = gs_ref[0:1, :]
    for k, at in enumerate(bands):
        raw = lax.dot_general(
            x_ref[:, at], g_ref[...], (((0,), (0,)), ((), ())), preferred_element_type=jnp.float32
        )
        grad = raw * group_scale
        for copy in loaded[3 + 3 * k : 6 + 3 * k]:
            copy.wait()
        moment_new = 0.9 * mo_ref[at, :] + 0.1 * grad
        second_new = 0.95 * se_ref[at, :] + 0.05 * grad * grad
        mo_v[k] = moment_new
        se_v[k] = second_new
        master = ma_ref[at, :]
        first_fix = moment_new * (1.0 / (1.0 - 0.9**8))
        second_fix = second_new * (1.0 / (1.0 - 0.95**8))
        ma_v[k] = master - 0.003 * (first_fix / (jnp.sqrt(second_fix) + 1e-08) + 0.1 * master)
        write(mo_v.at[k], mo_hbm.at[at, :])
        write(se_v.at[k], se_hbm.at[at, :])
        write(ma_v.at[k], ma_hbm.at[at, :])
    for copy in loaded[3 + 3 * len(bands) :]:
        copy.wait()
    ig_v[...] = sum_ref[...].astype(ig_v.dtype)
    ug_v[...] = up_ref[...].astype(ug_v.dtype)
    write(ig_v, ig_hbm)
    write(ug_v, ug_hbm)
    for copy in written:
        copy.wait()


def step(x_all, gate_all, input_scaled, up_scaled, group_scale, master, moment, second):
    states = master.shape
    bands = 4
    f32, bf16 = jnp.float32, jnp.bfloat16
    hbm = pl.BlockSpec(memory_space=pltpu.HBM)
    banded = pltpu.VMEM((bands, states[0] // bands, states[1]), f32)
    return pl.pallas_call(
        step_kernel,
        out_shape=(
            jax.ShapeDtypeStruct(input_scaled.shape, bf16),
            jax.ShapeDtypeStruct(up_scaled.shape, bf16),
        )
        + (jax.ShapeDtypeStruct(states, f32),) * 3,
        in_specs=[hbm] * 8,
        out_specs=(hbm,) * 5,
        scratch_shapes=[
            pltpu.VMEM(x_all.shape, bf16),
            pltpu.VMEM(gate_all.shape, bf16),
            pltpu.VMEM(input_scaled.shape, f32),
            pltpu.VMEM(up_scaled.shape, f32),
            pltpu.VMEM(group_scale.shape, f32),
            pltpu.VMEM(states, f32),
            pltpu.VMEM(states, f32),
            pltpu.VMEM(states, f32),
            pltpu.VMEM(input_scaled.shape, bf16),
            pltpu.VMEM(up_scaled.shape, bf16),
            banded,
            banded,
            banded,
            pltpu.SemaphoreType.DMA((5 + 3 * bands,)),
            pltpu.SemaphoreType.DMA((2 + 3 * bands,)),
        ],
        compiler_params=pltpu.CompilerParams(vmem_limit_bytes=54 * 1024 * 1024),
        name="step",
    )(x_all, gate_all, input_scaled, up_scaled, group_scale, master, moment, second)


def gather_path(
    inputs, gate_pre, up_pre, hidden_grad, segment_ids, doc_weight, w_gate, master, moment, second
):
    factors = exchange(inputs, gate_pre, up_pre, hidden_grad, segment_ids, doc_weight, w_gate)
    return step(*factors, master, moment, second)


def on_device(*args):
    inputs, gate_pre = args[:2]
    replicas, shards = lax.axis_size("replica"), lax.axis_size("shard")
    rows, features = inputs.shape
    hidden = gate_pre.shape[1]
    gathered = replicas * rows * (features // replicas + hidden)
    fits = rows % (QUARTERS * 32) == 0 and features % (replicas * 128) == 0
    if (replicas, shards) == (4, 8) and fits and gathered <= features * hidden:
        return gather_path(*args)
    return reduce_path(*args)


def solution(mesh):
    in_specs = (
        P("replica", None),
        P("replica", "shard"),
        P("replica", "shard"),
        P("replica", "shard"),
        P("replica", None),
        P("replica", None),
        P(None, "shard"),
        P("replica", "shard"),
        P("replica", "shard"),
        P("replica", "shard"),
    )
    out_specs = (
        P(("replica", "shard"), None),
        P("replica", "shard"),
        P("replica", "shard"),
        P("replica", "shard"),
        P("replica", "shard"),
    )
    return jax.shard_map(
        on_device, mesh=mesh, in_specs=in_specs, out_specs=out_specs, check_vma=False
    )
```

profile of v0, /device:TPU:0, one launch (start us, length us, event | category | flops | bytes accessed | tf_op | source)
XLA Modules:
  0.0 35.6 jit_solution(535847099508921299)
XLA Ops:
  0.6 28.2 %exchange.1 = (bf16[512,512]{1,0:T(8,128)(2,1)}, bf16[512,1024]{1,0:T(8,128)(2,1)}, f32[16,2048]{1,0:T(8,128)}, f32[128,1024]{1,0:T(8,128)}, f32[8,1024]{1,0:T(8,128)}) custom-call(bf16[128,2048]{1,0:T(8,128)(2,1)} %x_hbm.1, bf16[128,1024]{1,0:T(8,128)(2,1)} %gate_hbm.1, bf16[128,1024]{1,0:T(8,128)(2,1)} %up_hbm.1, bf16[128,1024]{1,0:T(8,128)(2,1)} %hid_hbm.1, ...), custom_call_target="tpu_custom_call" | custom-call | flops 536870912 | bytes 41943040 | tf_op jit(solution)/shard_map/exchange/pallas_call | solution.py:275
  28.8 6.8 %step.1 = (bf16[16,2048]{1,0:T(8,128)(2,1)}, bf16[128,1024]{1,0:T(8,128)(2,1)}, f32[512,1024]{1,0:T(8,128)}, f32[512,1024]{1,0:T(8,128)}, f32[512,1024]{1,0:T(8,128)}) custom-call(bf16[512,512]{1,0:T(8,128)(2,1)} %get-tuple-element.10.x_hbm, bf16[512,1024]{1,0:T(8,128)(2,1)} %get-tuple-element.11.g_hbm, f32[16,2048]{1,0:T(8,128)} %get-tuple-element.12.sum_hbm, ...), custom_call_target="tpu_custom_call" | custom-call | tf_op jit(solution)/shard_map/step/pallas_call | solution.py:386
where the time goes:
time: 35.7 us; the launch traced here: 35.6 us
  Pallas kernels  35 us (98%)
  between operations  0.64 us (2%)
    pallas_call x1, Pallas kernels, exchange(): pl.pallas_call(exchange_kernel, out_shape=(jax.ShapeDtypeStruct((replicas...  28.2 us
    pallas_call x1, Pallas kernels, step(): pl.pallas_call(step_kernel, out_shape=(jax.ShapeDtypeStruct(input_scaled....  6.77 us

commit v1 on v0

v1 whole, which is shorter than its diff:
```python
import functools

import jax
import jax.numpy as jnp
from jax import lax
from jax.experimental import pallas as pl
from jax.experimental.pallas import tpu as pltpu
from jax.sharding import PartitionSpec as P

MESH = pl.DeviceIdType.MESH
QUARTERS = 4
CHUNKS = 4
BAND = 64
LAYOUT = (7, 3, 5, 1, 6, 2, 4, 0)
KINDS = "hmhh"
X_LAST = ("mid", "near")
DONE = 3
ORDER = (
    "p0", "p1", "p2", "c2", "xc", "b1", "p3", "st0", "st1", "st2", "st3", "x0", "a2", "c3", "c0",
    "b0", "a0", "b2", "a3", "x1", "d1", "a1", "c1", "f2", "b3", "core", "xl0", "f3", "e0", "e2",
    "own", "xl1", "f0", "e1", "g0", "g2", "f1", "scale", "d0", "g1", "d2", "d3", "e3", "t0", "t1",
    "xe0", "xe1", "opt0", "g3", "t2", "opt1", "opt2", "i1", "i0", "i2", "t3", "i3",
)


def token_weights(segment_ids, doc_weight):
    labels = jnp.arange(doc_weight.shape[1], dtype=jnp.int32)
    onehot = segment_ids[:, :, None] == labels[None, None, :]
    return jnp.sum(jnp.where(onehot, doc_weight[:, None, :], 0), axis=2)


def adamw(grad, master, moment, second):
    moment_new = 0.9 * moment + 0.1 * grad
    second_new = 0.95 * second + 0.05 * grad * grad
    first_fix = moment_new / (1.0 - 0.9**8)
    second_fix = second_new / (1.0 - 0.95**8)
    master_new = master - 0.003 * (first_fix / (jnp.sqrt(second_fix) + 1e-08) + 0.1 * master)
    return master_new, moment_new, second_new


def reduce_path(
    inputs, gate_pre, up_pre, hidden_grad, segment_ids, doc_weight, w_gate, master, moment, second
):
    group_rows = inputs.shape[0]
    replicas = lax.axis_size("replica")
    weights = token_weights(segment_ids, doc_weight)[0]
    local_count = jnp.sum(weights)
    gate_f = gate_pre.astype(jnp.float32)
    sigmoid_gate = jax.nn.sigmoid(gate_f)
    weighted = hidden_grad.astype(jnp.float32) * weights.astype(jnp.float32)[:, None]
    gate_raw = (
        weighted * up_pre.astype(jnp.float32) * sigmoid_gate * (1.0 + gate_f * (1.0 - sigmoid_gate))
    ).astype(jnp.bfloat16)
    up_part = weighted * gate_f * sigmoid_gate
    input_part = lax.dot_general(
        gate_raw, w_gate, (((1,), (1,)), ((), ())), preferred_element_type=jnp.float32
    )
    input_summed = lax.psum_scatter(input_part, "shard", scatter_dimension=0, tiled=True)
    total = lax.psum(local_count, "replica").astype(jnp.float32)
    summed_grad = lax.psum_scatter(
        lax.dot_general(
            inputs, gate_raw, (((0,), (0,)), ((), ())), preferred_element_type=jnp.float32
        ),
        "replica",
        scatter_dimension=0,
        tiled=True,
    )
    scale = jnp.float32(group_rows * replicas) / total
    group_scale = jnp.float32(group_rows) / total
    input_grad = (input_summed * scale).astype(jnp.bfloat16)
    up_grad = (up_part * scale).astype(jnp.bfloat16)
    return (input_grad, up_grad) + adamw(summed_grad * group_scale, master, moment, second)


def flip(index, bit):
    return index + bit - 2 * bit * lax.rem(lax.div(index, bit), 2)


def exchange_kernel(
    x_hbm, gate_hbm, up_hbm, hid_hbm, seg_hbm, dw_hbm, w_hbm, ma_hbm, mo_hbm, se_hbm,
    ig_o, ug_o, gs_o, xt_o, gb, ma_o, mo_o, se_o,
    xs_v, xc_v, xg, gate_v, up_v, hid_v, seg_ref, dw_ref, w_v, xs32, xc32, xq, xp, tw_ref, gp, g32, gr, upo,
    part, rs_1, rs_2, cnt, cntr, dsum, lsem, wsem, tsem, ssem, rsem,
):
    r, s = lax.axis_index("replica"), lax.axis_index("shard")
    replicas = lax.axis_size("replica")
    core, side, across = flip(r, 1), flip(r, 2), flip(flip(r, 1), 2)
    near, mid, far = flip(s, 1), flip(s, 2), flip(s, 4)
    mid_far = flip(mid, 4)
    rows, width = gate_v.shape[0], xc_v.shape[1]
    quarter, tall = rows // QUARTERS, rows // 8
    chunk, span = gb.shape[2], part.shape[2]
    f32, bf16 = jnp.float32, jnp.bfloat16
    q = lax.rem(s, QUARTERS)

    def at_quarter(index):
        return pl.ds(pl.multiple_of(index * quarter, quarter), quarter)

    def columns(owner):
        return pl.ds(pl.multiple_of(owner * width, width), width)

    def load(src, dst, sem):
        copy = pltpu.make_async_copy(src, dst, sem)
        copy.start()
        return copy

    l_seg = load(seg_hbm, seg_ref, lsem.at[0])
    l_dw = load(dw_hbm, dw_ref, lsem.at[1])
    l_xs = load(x_hbm.at[at_quarter(q), columns(side)], xs_v.at[0], lsem.at[2])
    l_xa = load(x_hbm.at[at_quarter(q), columns(across)], xs_v.at[1], lsem.at[3])
    l_gate = load(gate_hbm, gate_v, lsem.at[4])
    l_hid = load(hid_hbm, hid_v, lsem.at[5])
    l_up = load(up_hbm, up_v, lsem.at[6])
    l_w = [
        load(w_hbm.at[pl.ds(c * span, span), :], w_v.at[pl.ds(c * span, span), :], wsem.at[c])
        for c in range(CHUNKS)
    ]
    l_xc = load(x_hbm.at[:, columns(core)], xc_v, lsem.at[7])
    l_xo = load(x_hbm.at[:, columns(r)], xg.at[pl.ds(0, rows), :], lsem.at[8])
    barrier = pltpu.get_barrier_semaphore()
    peers = [(core, s), (side, s), (across, s), (r, near), (r, mid), (r, far)]
    if "x" in KINDS:
        peers.append((r, mid_far))
    for peer in peers:
        pl.semaphore_signal(barrier, inc=1, device_id=peer, device_id_type=MESH)

    started = []

    def push(src, dst, peer):
        k = len(started)
        copy = pltpu.make_async_remote_copy(
            src_ref=src, dst_ref=dst, send_sem=ssem.at[k], recv_sem=rsem.at[k],
            device_id=peer, device_id_type=MESH,
        )
        copy.start()
        started.append(copy)
        return copy

    l_seg.wait()
    l_dw.wait()
    docs = dw_ref.shape[1]
    seg = jnp.broadcast_to(seg_ref[...].astype(f32), (128, rows)).T[:, :docs]
    labels = lax.broadcasted_iota(jnp.int32, (rows, docs), 1).astype(f32)
    dw = jnp.broadcast_to(dw_ref[...].astype(f32), (rows, docs))
    tw = jnp.sum(jnp.where(seg == labels, dw, 0.0), axis=1, keepdims=True)
    tw_ref[...] = jnp.broadcast_to(tw, tw_ref.shape)
    cnt[...] = jnp.broadcast_to(jnp.sum(tw, axis=0, keepdims=True), cnt.shape)

    l_xs.wait()
    xs32[0] = xs_v[0].astype(f32)
    l_xa.wait()
    xs32[1] = xs_v[1].astype(f32)
    pl.semaphore_wait(barrier, len(peers))
    x_first = [push(xs32.at[0], xq.at[0, 0], (side, s)), push(xs32.at[1], xq.at[1, 0], (across, s))]

    for copy in (l_gate, l_hid, l_up):
        copy.wait()
    g_side, g_core = [], []
    for k in range(CHUNKS):
        for j in range(chunk // 128):
            at, to = pl.ds(k * chunk + j * 128, 128), pl.ds(j * 128, 128)
            g = gate_v[:, at].astype(f32)
            sig = jax.nn.sigmoid(g)
            h = hid_v[:, at].astype(f32) * tw_ref[...]
            raw = (h * up_v[:, at].astype(f32) * sig * (1.0 + g * (1.0 - sig))).astype(bf16)
            upo[:, at] = h * g * sig
            gb[k, pl.ds(0, rows), to] = raw
            g32[k, :, to] = raw.astype(f32)
        g_side.append(push(g32.at[k], gr.at[1, k], (side, s)))
        if k == 0:
            counts = [push(cnt, cntr.at[n], (peer, s)) for n, peer in enumerate((core, side, across))]
        g_core.append(push(g32.at[k], gr.at[0, k], (core, s)))

    for n, position in enumerate(LAYOUT):
        block = s
        for bit in (1, 2, 4):
            if position & bit:
                block = flip(block, bit)
        at = pl.ds(pl.multiple_of(block * tall, tall), tall)
        for k in range(CHUNKS):
            gp[pl.ds(n * tall, tall), pl.ds(k * chunk, chunk)] = gb[k, at, :]

    first, second, states = {}, {}, {}

    def block(c, position):
        return part.at[c, pl.ds(LAYOUT.index(position) * tall, tall), :]

    def first_dim(c):
        return ((r, mid), 2) if KINDS[c] == "m" else ((r, near), 1)

    def second_dim(c):
        return ((r, near), 1) if KINDS[c] == "m" else ((r, mid), 2)

    def send_first(c, n):
        peer, bit = first_dim(c)
        position = bit + ((7 - bit, 3 - bit, 4, 0)[n])
        first[c, n] = push(block(c, position), rs_1.at[c, n], peer)

    def project(c):
        l_w[c].wait()
        part[c] = lax.dot_general(
            gp[...], w_v[pl.ds(c * span, span), :], (((1,), (1,)), ((), ())), preferred_element_type=f32
        )
        send_first(c, 0)

    def fetch(k):
        at = pl.ds(k * chunk, chunk)
        states[k] = [
            load(old.at[:, at], new.at[k], tsem.at[3 * k + n])
            for n, (old, new) in enumerate(((mo_hbm, mo_o), (se_hbm, se_o), (ma_hbm, ma_o)))
        ]

    def step_xc():
        l_xc.wait()
        xc32[...] = xc_v[...].astype(f32)
        x_core.append(push(xc32, xp, (core, s)))

    def forward(c, n):
        peer, bit = second_dim(c)
        kept = block(c, bit + 4 * (1 - n))
        first[c, n].wait_recv()
        kept[...] = kept[...] + rs_1[c, n]
        if KINDS[c] == "x" and n == 0:
            peer = (r, mid_far)
        second[c, n] = push(kept, rs_2.at[c, n], peer)

    def forward_far(c):
        kept = block(c, 4)
        first[c, 2].wait_recv()
        value = kept[...] + rs_1[c, 2]
        if KINDS[c] != "x":
            second[c, 0].wait_recv()
            value = value + rs_2[c, 0]
        kept[...] = value
        second[c, 2] = push(kept, rs_2.at[c, 2], (r, far))

    def finish(c):
        first[c, 3].wait_recv()
        total = block(c, 0)[...] + rs_1[c, 3]
        for n in (0, 1, 2) if KINDS[c] == "x" else (1, 2):
            second[c, n].wait_recv()
            total = total + rs_2[c, n]
        ig_o[:, pl.ds(c * span, span)] = (total * scale[0]).astype(bf16)

    def keep_x(group, slot, index):
        to = pl.ds(pl.multiple_of((group + 2) * rows + index * quarter, quarter), quarter)
        xg[to, :] = xq[group, slot].astype(bf16)

    def turn(group):
        xt_o[:, pl.ds(group * rows, rows)] = xg[pl.ds(group * rows, rows), :].T

    def step_x(group):
        x_first[group].wait_recv()
        x_near[group] = push(xq.at[group, 0], xq.at[group, 1], (r, near))
        x_mid[group] = push(xq.at[group, 0], xq.at[group, 2], (r, mid))
        keep_x(group, 0, q)

    def step_x_last(group):
        if X_LAST[group] == "mid":
            x_near[group].wait_recv()
            x_last[group] = push(xq.at[group, 1], xq.at[group, 3], (r, mid))
        else:
            x_mid[group].wait_recv()
            x_last[group] = push(xq.at[group, 2], xq.at[group, 3], (r, near))

    def step_x_end(group):
        if X_LAST[group] == "mid":
            x_mid[group].wait_recv()
        else:
            x_near[group].wait_recv()
        x_last[group].wait_recv()
        keep_x(group, 1, lax.rem(near, QUARTERS))
        keep_x(group, 2, lax.rem(mid, QUARTERS))
        keep_x(group, 3, lax.rem(flip(near, 2), QUARTERS))
        turn(group + 2)

    def step_own():
        l_xo.wait()
        turn(0)
        x_core[0].wait_recv()
        xg[pl.ds(rows, rows), :] = xp[...].astype(bf16)
        turn(1)

    def store_g(k, group):
        value = gr[group, k].astype(bf16)
        gb[k, pl.ds((group + 1) * rows, rows), :] = value

    def step_core():
        for k in range(CHUNKS):
            g_core[k].wait_recv()
            store_g(k, 0)

    def relay(k):
        g_side[k].wait_recv()
        g_across[k] = push(gr.at[1, k], gr.at[2, k], (core, s))
        store_g(k, 1)

    def step_scale():
        for copy in counts:
            copy.wait_recv()
        total = (cnt[...] + cntr[0] + cntr[1] + cntr[2])[0:1, 0:1]
        scale.append(f32(rows * replicas) / total)
        scale.append(f32(rows) / total)
        gs_o[...] = jnp.broadcast_to(scale[1], gs_o.shape)
        ug_o[...] = (upo[...] * scale[0]).astype(bf16)

    def take(k):
        g_across[k].wait_recv()
        store_g(k, 2)

    def optimize(k):
        dsum[...] = jnp.dot(xt_o[...], gb[k], preferred_element_type=f32)
        for copy in states[k]:
            copy.wait()
        for n in range(width // BAND):
            at = pl.ds(n * BAND, BAND)
            update(dsum[at, :] * scale[1], ma_o.at[k, at], mo_o.at[k, at], se_o.at[k, at],
                   ma_o.at[k, at], mo_o.at[k, at], se_o.at[k, at])

    x_core, x_near, x_mid, x_last, g_across, scale = [], {}, {}, {}, {}, []
    steps = {
        "xc": step_xc, "own": step_own, "core": step_core, "scale": step_scale, "x": step_x, "xl": step_x_last,
        "xe": step_x_end, "st": fetch, "p": project,
        "b": lambda c: send_first(c, 1), "c": lambda c: send_first(c, 2), "d": lambda c: send_first(c, 3),
        "a": lambda c: forward(c, 0), "e": lambda c: forward(c, 1), "f": forward_far, "i": finish, "g": relay, "t": take, "opt": optimize,
    }
    for name in ORDER:
        kind = name.rstrip("0123456789")
        index = name[len(kind):]
        steps[kind](*([int(index)] if index else []))
    for k in range(DONE, CHUNKS):
        for copy in states[k]:
            copy.wait()
    for copy in started:
        copy.wait_send()


def update(grad, ma, mo, se, ma_to, mo_to, se_to):
    moment_new = 0.9 * mo[...] + 0.1 * grad
    second_new = 0.95 * se[...] + 0.05 * grad * grad
    master = ma[...]
    mo_to[...] = moment_new
    se_to[...] = second_new
    first_fix = moment_new * (1.0 / (1.0 - 0.9**8))
    second_fix = second_new * (1.0 / (1.0 - 0.95**8))
    ma_to[...] = master - 0.003 * (first_fix / (jnp.sqrt(second_fix) + 1e-08) + 0.1 * master)


def exchange(inputs, gate_pre, up_pre, hidden_grad, segment_ids, doc_weight, w_gate, master, moment, second):
    replicas, shards = lax.axis_size("replica"), lax.axis_size("shard")
    rows, features = inputs.shape
    hidden = gate_pre.shape[1]
    width, tall, quarter = features // replicas, rows // shards, rows // QUARTERS
    chunk, span = hidden // CHUNKS, features // CHUNKS
    f32, bf16 = jnp.float32, jnp.bfloat16
    hbm = pl.BlockSpec(memory_space=pltpu.HBM)
    vmem = pl.BlockSpec(memory_space=pltpu.VMEM)
    copies = 2 + 3 + 2 * CHUNKS + 1 + 6 + CHUNKS + 7 * CHUNKS
    state = pltpu.VMEM((CHUNKS, width, chunk), f32)
    operands = (inputs, gate_pre, up_pre, hidden_grad, segment_ids, doc_weight, w_gate, master, moment, second)
    return pl.pallas_call(
        exchange_kernel,
        out_shape=(
            pltpu.VMEM((tall, features), bf16),
            pltpu.VMEM((rows, hidden), bf16),
            pltpu.VMEM((8, chunk), f32),
            pltpu.VMEM((width, replicas * rows), bf16),
            pltpu.VMEM((CHUNKS, replicas * rows, chunk), bf16),
            state,
            state,
            state,
        ),
        in_specs=[hbm] * 10,
        out_specs=(vmem,) * 8,
        scratch_shapes=[
            pltpu.VMEM((2, quarter, width), bf16),
            pltpu.VMEM((rows, width), bf16),
            pltpu.VMEM((replicas * rows, width), bf16),
            pltpu.VMEM((rows, hidden), bf16),
            pltpu.VMEM((rows, hidden), bf16),
            pltpu.VMEM((rows, hidden), bf16),
            pltpu.VMEM(segment_ids.shape, jnp.int32),
            pltpu.VMEM(doc_weight.shape, jnp.int32),
            pltpu.VMEM((features, hidden), bf16),
            pltpu.VMEM((2, quarter, width), f32),
            pltpu.VMEM((rows, width), f32),
            pltpu.VMEM((2, QUARTERS, quarter, width), f32),
            pltpu.VMEM((rows, width), f32),
            pltpu.VMEM((rows, 128), f32),
            pltpu.VMEM((rows, hidden), bf16),
            pltpu.VMEM((CHUNKS, rows, chunk), f32),
            pltpu.VMEM((3, CHUNKS, rows, chunk), f32),
            pltpu.VMEM((rows, hidden), f32),
            pltpu.VMEM((CHUNKS, rows, span), f32),
            pltpu.VMEM((CHUNKS, 4, tall, span), f32),
            pltpu.VMEM((CHUNKS, 3, tall, span), f32),
            pltpu.VMEM((8, 128), f32),
            pltpu.VMEM((3, 8, 128), f32),
            pltpu.VMEM((width, chunk), f32),
            pltpu.SemaphoreType.DMA((9,)),
            pltpu.SemaphoreType.DMA((CHUNKS,)),
            pltpu.SemaphoreType.DMA((3 * CHUNKS,)),
            pltpu.SemaphoreType.DMA((copies,)),
            pltpu.SemaphoreType.DMA((copies,)),
        ],
        compiler_params=pltpu.CompilerParams(
            collective_id=0, has_side_effects=True, vmem_limit_bytes=40 * 1024 * 1024
        ),
        cost_estimate=pl.CostEstimate(
            flops=4 * rows * hidden * features, bytes_accessed=12 * 1024 * 1024, transcendentals=0
        ),
        name="exchange",
    )(*[pltpu.with_memory_space_constraint(operand, pltpu.HBM) for operand in operands])


def step_kernel(
    ig_ref, ug_ref, gs_ref, xt_ref, gb_ref, ma_ref, mo_ref, se_ref,
    ig_hbm, ug_hbm, ma_hbm, mo_hbm, se_hbm,
    ma_v, mo_v, se_v, sems,
):
    written = []
    chunks, width, chunk = ma_ref.shape

    def write(src, dst):
        copy = pltpu.make_async_copy(src, dst, sems.at[len(written)])
        copy.start()
        written.append(copy)

    for k in range(DONE):
        for src, dst in ((mo_ref, mo_hbm), (se_ref, se_hbm), (ma_ref, ma_hbm)):
            write(src.at[k], dst.at[:, pl.ds(k * chunk, chunk)])
    write(ig_ref, ig_hbm)
    write(ug_ref, ug_hbm)
    group_scale = gs_ref[0:1, :]
    half = width // 2
    for k in range(DONE, chunks):
        for m in range(2):
            rows = pl.ds(m * half, half)
            raw = jnp.dot(xt_ref[rows, :], gb_ref[k], preferred_element_type=jnp.float32)
            mo_v[k - DONE, rows, :] = raw * group_scale
            for n in range(half // BAND):
                at = pl.ds(m * half + n * BAND, BAND)
                update(mo_v[k - DONE, at, :], ma_ref.at[k, at], mo_ref.at[k, at], se_ref.at[k, at],
                       ma_v.at[k - DONE, at], mo_v.at[k - DONE, at], se_v.at[k - DONE, at])
            for src, dst in ((mo_v, mo_hbm), (se_v, se_hbm), (ma_v, ma_hbm)):
                write(src.at[k - DONE, rows], dst.at[rows, pl.ds(k * chunk, chunk)])
    for copy in written:
        copy.wait()


def step(ig, ug, gs, xt, gb, ma, mo, se):
    chunks, width, chunk = ma.shape
    f32 = jnp.float32
    hbm = pl.BlockSpec(memory_space=pltpu.HBM)
    vmem = pl.BlockSpec(memory_space=pltpu.VMEM)
    late = pltpu.VMEM((chunks - DONE, width, chunk), f32)
    return pl.pallas_call(
        step_kernel,
        out_shape=(
            jax.ShapeDtypeStruct(ig.shape, ig.dtype),
            jax.ShapeDtypeStruct(ug.shape, ug.dtype),
        )
        + (jax.ShapeDtypeStruct((width, chunks * chunk), f32),) * 3,
        in_specs=[vmem] * 8,
        out_specs=(hbm,) * 5,
        scratch_shapes=[late, late, late, pltpu.SemaphoreType.DMA((2 + 3 * DONE + 6 * (chunks - DONE),))],
        compiler_params=pltpu.CompilerParams(vmem_limit_bytes=40 * 1024 * 1024),
        name="step",
    )(ig, ug, gs, xt, gb, ma, mo, se)


def gather_path(*args):
    return step(*exchange(*args))


def on_device(*args):
    inputs, gate_pre = args[:2]
    replicas, shards = lax.axis_size("replica"), lax.axis_size("shard")
    rows, features = inputs.shape
    hidden = gate_pre.shape[1]
    gathered = replicas * rows * (features // replicas + hidden)
    fits = rows % (QUARTERS * 32) == 0 and features % (replicas * 128) == 0 and hidden % (CHUNKS * 128) == 0
    if (replicas, shards) == (4, 8) and fits and gathered <= features * hidden:
        return gather_path(*args)
    return reduce_path(*args)


def solution(mesh):
    in_specs = (
        P("replica", None),
        P("replica", "shard"),
        P("replica", "shard"),
        P("replica", "shard"),
        P("replica", None),
        P("replica", None),
        P(None, "shard"),
        P("replica", "shard"),
        P("replica", "shard"),
        P("replica", "shard"),
    )
    out_specs = (
        P(("replica", "shard"), None),
        P("replica", "shard"),
        P("replica", "shard"),
        P("replica", "shard"),
        P("replica", "shard"),
    )
    return jax.shard_map(
        on_device, mesh=mesh, in_specs=in_specs, out_specs=out_specs, check_vma=False
    )
```

time: 35.7 us -> 29.1 us (0.82)
  Pallas kernels: 35 us -> 28.3 us
    pallas_call x2, Pallas kernels: 35 us -> 28.3 us  [the longest x1 25.4 us: exchange(): pl.pallas_call(exchange_kernel, out_shape=(pltpu.VMEM((tall, features), b...]
where the time goes in v1:
time: 29.1 us; the launch traced here: 29 us
  Pallas kernels  28.3 us (97%)
  between operations  0.64 us (2%)
    pallas_call x1, Pallas kernels, exchange(): pl.pallas_call(exchange_kernel, out_shape=(pltpu.VMEM((tall, features), b...  25.4 us
    pallas_call x1, Pallas kernels, step(): pl.pallas_call(step_kernel, out_shape=(jax.ShapeDtypeStruct(ig.shape, ig....  2.9 us

profile of v1, /device:TPU:0, one launch (start us, length us, event | category | flops | bytes accessed | tf_op | source)
XLA Modules:
  0.0 29.0 jit_solution(3538774510474255314)
XLA Ops:
  0.6 25.4 %exchange.1 = (bf16[16,2048]{1,0:T(8,128)(2,1)S(1)}, bf16[128,1024]{1,0:T(8,128)(2,1)S(1)}, f32[8,256]{1,0:T(8,128)S(1)}, bf16[512,512]{1,0:T(8,128)(2,1)S(1)}, ...) custom-call(bf16[128,2048]{1,0:T(8,128)(2,1)} %x_hbm.1, ...), custom_call_target="tpu_custom_call" | custom-call | flops 1073741824 | bytes 12582912 | tf_op jit(solution)/shard_map/exchange/pallas_call | solution.py:361
  26.1 2.9 %step.1 = (bf16[16,2048]{1,0:T(8,128)(2,1)}, bf16[128,1024]{1,0:T(8,128)(2,1)}, f32[512,1024]{1,0:T(8,128)}, f32[512,1024]{1,0:T(8,128)}, f32[512,1024]{1,0:T(8,128)}) custom-call(bf16[16,2048]{1,0:T(8,128)(2,1)S(1)} %get-tuple-element.13.ig_ref, bf16[128,1024]{1,0:T(8,128)(2,1)S(1)} %get-tuple-element.14.ug_ref, f32[8,256]{1,0:T(8,128)S(1)} %get-tuple-element.15.gs_ref, ...), custom_call_target="tpu_custom_call" | custom-call | tf_op jit(solution)/shard_map/step/pallas_call | solution.py:457

commit v2 on v1

--- a/solution.py
+++ b/solution.py
@@ -12,14 +12,14 @@
 CHUNKS = 4
 BAND = 64
 LAYOUT = (7, 3, 5, 1, 6, 2, 4, 0)
-KINDS = "hmhh"
-X_LAST = ("mid", "near")
+KINDS = "mhmh"
+X_LAST = ("near", "near")
 DONE = 3
 ORDER = (
-    "p0", "p1", "p2", "c2", "xc", "b1", "p3", "st0", "st1", "st2", "st3", "x0", "a2", "c3", "c0",
-    "b0", "a0", "b2", "a3", "x1", "d1", "a1", "c1", "f2", "b3", "core", "xl0", "f3", "e0", "e2",
-    "own", "xl1", "f0", "e1", "g0", "g2", "f1", "scale", "d0", "g1", "d2", "d3", "e3", "t0", "t1",
-    "xe0", "xe1", "opt0", "g3", "t2", "opt1", "opt2", "i1", "i0", "i2", "t3", "i3",
+    "p2", "p1", "c1", "b2", "p0", "b1", "b0", "p3", "st0", "st1", "st2", "st3", "xc", "c0", "b3",
+    "x1", "a2", "c2", "a1", "x0", "a3", "c3", "a0", "e3", "g0", "d0", "f1", "xl1", "own", "xl0",
+    "f2", "d2", "e1", "t0", "f0", "e0", "f3", "g1", "core", "xe1", "scale", "d1", "d3", "e2", "t1",
+    "g2", "xe0", "opt0", "opt1", "t2", "g3", "opt2", "i0", "i2", "i1", "i3", "t3",
 )
 
 
@@ -104,6 +104,13 @@
         copy.start()
         return copy
 
+    barrier = pltpu.get_barrier_semaphore()
+    peers = [(core, s), (side, s), (across, s), (r, near), (r, mid), (r, far)]
+    if "x" in KINDS:
+        peers.append((r, mid_far))
+    for peer in peers:
+        pl.semaphore_signal(barrier, inc=1, device_id=peer, device_id_type=MESH)
+
     l_seg = load(seg_hbm, seg_ref, lsem.at[0])
     l_dw = load(dw_hbm, dw_ref, lsem.at[1])
     l_xs = load(x_hbm.at[at_quarter(q), columns(side)], xs_v.at[0], lsem.at[2])
@@ -117,13 +124,6 @@
     ]
     l_xc = load(x_hbm.at[:, columns(core)], xc_v, lsem.at[7])
     l_xo = load(x_hbm.at[:, columns(r)], xg.at[pl.ds(0, rows), :], lsem.at[8])
-    barrier = pltpu.get_barrier_semaphore()
-    peers = [(core, s), (side, s), (across, s), (r, near), (r, mid), (r, far)]
-    if "x" in KINDS:
-        peers.append((r, mid_far))
-    for peer in peers:
-        pl.semaphore_signal(barrier, inc=1, device_id=peer, device_id_type=MESH)
-
     started = []
 
     def push(src, dst, peer):
@@ -151,6 +151,7 @@
     l_xa.wait()
     xs32[1] = xs_v[1].astype(f32)
     pl.semaphore_wait(barrier, len(peers))
+    counts = [push(cnt, cntr.at[n], (peer, s)) for n, peer in enumerate((core, side, across))]
     x_first = [push(xs32.at[0], xq.at[0, 0], (side, s)), push(xs32.at[1], xq.at[1, 0], (across, s))]
 
     for copy in (l_gate, l_hid, l_up):
@@ -167,8 +168,6 @@
             gb[k, pl.ds(0, rows), to] = raw
             g32[k, :, to] = raw.astype(f32)
         g_side.append(push(g32.at[k], gr.at[1, k], (side, s)))
-        if k == 0:
-            counts = [push(cnt, cntr.at[n], (peer, s)) for n, peer in enumerate((core, side, across))]
         g_core.append(push(g32.at[k], gr.at[0, k], (core, s)))
 
     for n, position in enumerate(LAYOUT):

time: 29.1 us -> 26.7 us (0.918)
  Pallas kernels: 28.3 us -> 25.9 us
    pallas_call x1, Pallas kernels: 25.4 us -> 23 us  [exchange(): pl.pallas_call(exchange_kernel, out_shape=(pltpu.VMEM((tall, features), b...]
where the time goes in v2:
time: 26.7 us; the launch traced here: 26.6 us
  Pallas kernels  25.9 us (97%)
  between operations  0.64 us (2%)
    pallas_call x1, Pallas kernels, exchange(): pl.pallas_call(exchange_kernel, out_shape=(pltpu.VMEM((tall, features), b...  23 us
    pallas_call x1, Pallas kernels, step(): pl.pallas_call(step_kernel, out_shape=(jax.ShapeDtypeStruct(ig.shape, ig....  2.9 us

profile of v2, /device:TPU:0, one launch (start us, length us, event | category | flops | bytes accessed | tf_op | source)
XLA Modules:
  0.0 26.6 jit_solution(5012764437711860678)
XLA Ops:
  0.6 23.0 %exchange.1 = (bf16[16,2048]{1,0:T(8,128)(2,1)S(1)}, bf16[128,1024]{1,0:T(8,128)(2,1)S(1)}, f32[8,256]{1,0:T(8,128)S(1)}, bf16[512,512]{1,0:T(8,128)(2,1)S(1)}, ...) custom-call(bf16[128,2048]{1,0:T(8,128)(2,1)} %x_hbm.1, ...), custom_call_target="tpu_custom_call" | custom-call | flops 1073741824 | bytes 12582912 | tf_op jit(solution)/shard_map/exchange/pallas_call | solution.py:360
  23.7 2.9 %step.1 = (bf16[16,2048]{1,0:T(8,128)(2,1)}, bf16[128,1024]{1,0:T(8,128)(2,1)}, f32[512,1024]{1,0:T(8,128)}, f32[512,1024]{1,0:T(8,128)}, f32[512,1024]{1,0:T(8,128)}) custom-call(bf16[16,2048]{1,0:T(8,128)(2,1)S(1)} %get-tuple-element.13.ig_ref, bf16[128,1024]{1,0:T(8,128)(2,1)S(1)} %get-tuple-element.14.ug_ref, f32[8,256]{1,0:T(8,128)S(1)} %get-tuple-element.15.gs_ref, ...), custom_call_target="tpu_custom_call" | custom-call | tf_op jit(solution)/shard_map/step/pallas_call | solution.py:456

commit v3 on v2

--- a/solution.py
+++ b/solution.py
@@ -16,11 +16,12 @@
 X_LAST = ("near", "near")
 DONE = 3
 ORDER = (
-    "p2", "p1", "c1", "b2", "p0", "b1", "b0", "p3", "st0", "st1", "st2", "st3", "xc", "c0", "b3",
-    "x1", "a2", "c2", "a1", "x0", "a3", "c3", "a0", "e3", "g0", "d0", "f1", "xl1", "own", "xl0",
-    "f2", "d2", "e1", "t0", "f0", "e0", "f3", "g1", "core", "xe1", "scale", "d1", "d3", "e2", "t1",
-    "g2", "xe0", "opt0", "opt1", "t2", "g3", "opt2", "i0", "i2", "i1", "i3", "t3",
+    "p0", "p1", "c1", "d0", "b1", "c0", "xc", "p3", "p2", "tell", "st0", "st1", "st2", "st3", "b0",
+    "core", "x1", "a0", "c3", "a1", "x0", "e1", "a2", "c2", "a3", "far", "f0", "b3", "f1", "b2",
+    "xl1", "g0", "own", "xl0", "g1", "e0", "t1", "e3", "f3", "scale", "d1", "d3", "d2", "f2", "e2",
+    "g2", "xe1", "xe0", "t0", "opt0", "i0", "g3", "opt1", "t2", "i1", "opt2", "t3", "i3", "i2",
 )
+LATE = 0
 
 
 def token_weights(segment_ids, doc_weight):
@@ -80,13 +81,15 @@
     x_hbm, gate_hbm, up_hbm, hid_hbm, seg_hbm, dw_hbm, w_hbm, ma_hbm, mo_hbm, se_hbm,
     ig_o, ug_o, gs_o, xt_o, gb, ma_o, mo_o, se_o,
     xs_v, xc_v, xg, gate_v, up_v, hid_v, seg_ref, dw_ref, w_v, xs32, xc32, xq, xp, tw_ref, gp, g32, gr, upo,
-    part, rs_1, rs_2, cnt, cntr, dsum, lsem, wsem, tsem, ssem, rsem,
+    part, rs_1, rs_2, cnt, cntr, dsum, lsem, wsem, tsem, ssem, rsem, far_sem,
 ):
     r, s = lax.axis_index("replica"), lax.axis_index("shard")
     replicas = lax.axis_size("replica")
     core, side, across = flip(r, 1), flip(r, 2), flip(flip(r, 1), 2)
     near, mid, far = flip(s, 1), flip(s, 2), flip(s, 4)
     mid_far = flip(mid, 4)
+    inner = lax.rem(lax.rem(lax.div(s, 2), 2) + lax.div(s, 4), 2)
+    odd_core = lax.rem(r, 2)
     rows, width = gate_v.shape[0], xc_v.shape[1]
     quarter, tall = rows // QUARTERS, rows // 8
     chunk, span = gb.shape[2], part.shape[2]
@@ -105,11 +108,14 @@
         return copy
 
     barrier = pltpu.get_barrier_semaphore()
-    peers = [(core, s), (side, s), (across, s), (r, near), (r, mid), (r, far)]
-    if "x" in KINDS:
-        peers.append((r, mid_far))
+    peers = [(core, s), (side, s), (across, s), (r, near), (r, mid)]
     for peer in peers:
         pl.semaphore_signal(barrier, inc=1, device_id=peer, device_id_type=MESH)
+
+    @pl.when(inner == 1)
+    def greet_inner():
+        pl.semaphore_signal(barrier, inc=1, device_id=(r, mid_far), device_id_type=MESH)
+
 
     l_seg = load(seg_hbm, seg_ref, lsem.at[0])
     l_dw = load(dw_hbm, dw_ref, lsem.at[1])
@@ -124,17 +130,28 @@
     ]
     l_xc = load(x_hbm.at[:, columns(core)], xc_v, lsem.at[7])
     l_xo = load(x_hbm.at[:, columns(r)], xg.at[pl.ds(0, rows), :], lsem.at[8])
-    started = []
-
-    def push(src, dst, peer):
-        k = len(started)
+    started, by_odd, made = [], [], []
+
+    def make(src, dst, peer, kept):
+        k = len(made)
         copy = pltpu.make_async_remote_copy(
             src_ref=src, dst_ref=dst, send_sem=ssem.at[k], recv_sem=rsem.at[k],
             device_id=peer, device_id_type=MESH,
         )
+        made.append(copy)
+        kept.append(copy)
+        return copy
+
+    def push(src, dst, peer):
+        copy = make(src, dst, peer, started)
         copy.start()
-        started.append(copy)
         return copy
+
+    def when_odd(action):
+        pl.when(odd_core == 1)(action)
+
+    def when_even(action):
+        pl.when(odd_core == 0)(action)
 
     l_seg.wait()
     l_dw.wait()
@@ -150,7 +167,7 @@
     xs32[0] = xs_v[0].astype(f32)
     l_xa.wait()
     xs32[1] = xs_v[1].astype(f32)
-    pl.semaphore_wait(barrier, len(peers))
+    pl.semaphore_wait(barrier, len(peers) + inner)
     counts = [push(cnt, cntr.at[n], (peer, s)) for n, peer in enumerate((core, side, across))]
     x_first = [push(xs32.at[0], xq.at[0, 0], (side, s)), push(xs32.at[1], xq.at[1, 0], (across, s))]
 
@@ -167,7 +184,11 @@
             upo[:, at] = h * g * sig
             gb[k, pl.ds(0, rows), to] = raw
             g32[k, :, to] = raw.astype(f32)
-        g_side.append(push(g32.at[k], gr.at[1, k], (side, s)))
+        if k < CHUNKS - LATE:
+            g_side.append(push(g32.at[k], gr.at[1, k], (side, s)))
+        else:
+            g_side.append(make(g32.at[k], gr.at[1, k], (side, s), by_odd))
+            when_odd(g_side[k].start)
         g_core.append(push(g32.at[k], gr.at[0, k], (core, s)))
 
     for n, position in enumerate(LAYOUT):
@@ -219,24 +240,28 @@
         kept = block(c, bit + 4 * (1 - n))
         first[c, n].wait_recv()
         kept[...] = kept[...] + rs_1[c, n]
-        if KINDS[c] == "x" and n == 0:
-            peer = (r, mid_far)
         second[c, n] = push(kept, rs_2.at[c, n], peer)
+
+    def open_far():
+        pl.semaphore_wait(far_sem, 1)
+
+    def announce():
+        @pl.when(inner == 1)
+        def tell():
+            for peer in ((r, mid), (r, mid_far)):
+                pl.semaphore_signal(far_sem, inc=1, device_id=peer, device_id_type=MESH)
 
     def forward_far(c):
         kept = block(c, 4)
         first[c, 2].wait_recv()
-        value = kept[...] + rs_1[c, 2]
-        if KINDS[c] != "x":
-            second[c, 0].wait_recv()
-            value = value + rs_2[c, 0]
-        kept[...] = value
+        second[c, 0].wait_recv()
+        kept[...] = kept[...] + rs_1[c, 2] + rs_2[c, 0]
         second[c, 2] = push(kept, rs_2.at[c, 2], (r, far))
 
     def finish(c):
         first[c, 3].wait_recv()
         total = block(c, 0)[...] + rs_1[c, 3]
-        for n in (0, 1, 2) if KINDS[c] == "x" else (1, 2):
+        for n in (1, 2):
             second[c, n].wait_recv()
             total = total + rs_2[c, n]
         ig_o[:, pl.ds(c * span, span)] = (total * scale[0]).astype(bf16)
@@ -286,10 +311,37 @@
 
     def step_core():
         for k in range(CHUNKS):
-            g_core[k].wait_recv()
+            if k < CHUNKS - LATE:
+                g_core[k].wait_recv()
+            else:
+                when_even(g_core[k].wait_recv)
             store_g(k, 0)
 
+    def lend():
+        for k in range(CHUNKS - LATE, CHUNKS):
+            g_lent[k] = make(gr.at[0, k], gr.at[2, k], (side, s), by_odd)
+            g_across[k] = make(gr.at[1, k], gr.at[2, k], (core, s), by_odd)
+            g_back[k] = make(gr.at[2, k], gr.at[1, k], (core, s), by_odd)
+
+        def send():
+            for k in range(CHUNKS - LATE, CHUNKS):
+                g_core[k].wait_recv()
+                g_lent[k].start()
+
+        when_odd(send)
+
     def relay(k):
+        if k >= CHUNKS - LATE:
+            def both():
+                g_side[k].wait_recv()
+                g_across[k].start()
+                g_lent[k].wait_recv()
+                g_back[k].start()
+                store_g(k, 1)
+                store_g(k, 2)
+
+            when_odd(both)
+            return
         g_side[k].wait_recv()
         g_across[k] = push(gr.at[1, k], gr.at[2, k], (core, s))
         store_g(k, 1)
@@ -304,6 +356,15 @@
         ug_o[...] = (upo[...] * scale[0]).astype(bf16)
 
     def take(k):
+        if k >= CHUNKS - LATE:
+            def both():
+                g_across[k].wait_recv()
+                g_back[k].wait_recv()
+                store_g(k, 1)
+                store_g(k, 2)
+
+            when_even(both)
+            return
         g_across[k].wait_recv()
         store_g(k, 2)
 
@@ -316,10 +377,10 @@
             update(dsum[at, :] * scale[1], ma_o.at[k, at], mo_o.at[k, at], se_o.at[k, at],
                    ma_o.at[k, at], mo_o.at[k, at], se_o.at[k, at])
 
-    x_core, x_near, x_mid, x_last, g_across, scale = [], {}, {}, {}, {}, []
+    x_core, x_near, x_mid, x_last, g_across, g_lent, g_back, scale = [], {}, {}, {}, {}, {}, {}, []
     steps = {
         "xc": step_xc, "own": step_own, "core": step_core, "scale": step_scale, "x": step_x, "xl": step_x_last,
-        "xe": step_x_end, "st": fetch, "p": project,
+        "xe": step_x_end, "st": fetch, "p": project, "lend": lend, "tell": announce, "far": open_far,
         "b": lambda c: send_first(c, 1), "c": lambda c: send_first(c, 2), "d": lambda c: send_first(c, 3),
         "a": lambda c: forward(c, 0), "e": lambda c: forward(c, 1), "f": forward_far, "i": finish, "g": relay, "t": take, "opt": optimize,
     }
@@ -333,6 +394,12 @@
     for copy in started:
         copy.wait_send()
 
+    def wait_odd():
+        for copy in by_odd:
+            copy.wait_send()
+
+    when_odd(wait_odd)
+
 
 def update(grad, ma, mo, se, ma_to, mo_to, se_to):
     moment_new = 0.9 * mo[...] + 0.1 * grad
@@ -354,7 +421,7 @@
     f32, bf16 = jnp.float32, jnp.bfloat16
     hbm = pl.BlockSpec(memory_space=pltpu.HBM)
     vmem = pl.BlockSpec(memory_space=pltpu.VMEM)
-    copies = 2 + 3 + 2 * CHUNKS + 1 + 6 + CHUNKS + 7 * CHUNKS
+    copies = 2 + 3 + 2 * CHUNKS + 1 + 6 + CHUNKS + 7 * CHUNKS + 2 * LATE
     state = pltpu.VMEM((CHUNKS, width, chunk), f32)
     operands = (inputs, gate_pre, up_pre, hidden_grad, segment_ids, doc_weight, w_gate, master, moment, second)
     return pl.pallas_call(
@@ -401,6 +468,7 @@
             pltpu.SemaphoreType.DMA((3 * CHUNKS,)),
             pltpu.SemaphoreType.DMA((copies,)),
             pltpu.SemaphoreType.DMA((copies,)),
+            pltpu.SemaphoreType.REGULAR,
         ],
         compiler_params=pltpu.CompilerParams(
             collective_id=0, has_side_effects=True, vmem_limit_bytes=40 * 1024 * 1024

time: 26.7 us -> 26.4 us (0.989)
  Pallas kernels: 25.9 us -> 25.4 us
    pallas_call x1, Pallas kernels: 23 us -> 22.5 us  [exchange(): pl.pallas_call(exchange_kernel, out_shape=(pltpu.VMEM((tall, features), b...]
where the time goes in v3:
time: 26.4 us; the launch traced here: 26 us
  Pallas kernels  25.4 us (96%)
  between operations  0.64 us (2%)
    pallas_call x1, Pallas kernels, exchange(): pl.pallas_call(exchange_kernel, out_shape=(pltpu.VMEM((tall, features), b...  22.5 us
    pallas_call x1, Pallas kernels, step(): pl.pallas_call(step_kernel, out_shape=(jax.ShapeDtypeStruct(ig.shape, ig....  2.9 us

profile of v3, /device:TPU:0, one launch (start us, length us, event | category | flops | bytes accessed | tf_op | source)
XLA Modules:
  0.0 26.0 jit_solution(17635059702834308254)
XLA Ops:
  0.6 22.5 %exchange.1 = (bf16[16,2048]{1,0:T(8,128)(2,1)S(1)}, bf16[128,1024]{1,0:T(8,128)(2,1)S(1)}, f32[8,256]{1,0:T(8,128)S(1)}, bf16[512,512]{1,0:T(8,128)(2,1)S(1)}, ...) custom-call(bf16[128,2048]{1,0:T(8,128)(2,1)} %x_hbm.1, ...), custom_call_target="tpu_custom_call" | custom-call | flops 1073741824 | bytes 12582912 | tf_op jit(solution)/shard_map/exchange/pallas_call | solution.py:427
  23.1 2.9 %step.1 = (bf16[16,2048]{1,0:T(8,128)(2,1)}, bf16[128,1024]{1,0:T(8,128)(2,1)}, f32[512,1024]{1,0:T(8,128)}, f32[512,1024]{1,0:T(8,128)}, f32[512,1024]{1,0:T(8,128)}) custom-call(bf16[16,2048]{1,0:T(8,128)(2,1)S(1)} %get-tuple-element.13.ig_ref, bf16[128,1024]{1,0:T(8,128)(2,1)S(1)} %get-tuple-element.14.ug_ref, f32[8,256]{1,0:T(8,128)S(1)} %get-tuple-element.15.gs_ref, ...), custom_call_target="tpu_custom_call" | custom-call | tf_op jit(solution)/shard_map/step/pallas_call | solution.py:524

commit v4 on v2

--- a/solution.py
+++ b/solution.py
@@ -16,10 +16,10 @@
 X_LAST = ("near", "near")
 DONE = 3
 ORDER = (
-    "p2", "p1", "c1", "b2", "p0", "b1", "b0", "p3", "st0", "st1", "st2", "st3", "xc", "c0", "b3",
-    "x1", "a2", "c2", "a1", "x0", "a3", "c3", "a0", "e3", "g0", "d0", "f1", "xl1", "own", "xl0",
-    "f2", "d2", "e1", "t0", "f0", "e0", "f3", "g1", "core", "xe1", "scale", "d1", "d3", "e2", "t1",
-    "g2", "xe0", "opt0", "opt1", "t2", "g3", "opt2", "i0", "i2", "i1", "i3", "t3",
+    "p0", "pass", "p1", "xc", "c0", "p3", "p2", "st0", "st1", "st2", "st3", "c2", "b3", "c1", "b2",
+    "b1", "a0", "x1", "a1", "a2", "x0", "b0", "c3", "a3", "e1", "far", "f1", "core", "d0", "scale",
+    "e3", "d2", "own", "f0", "xl1", "f2", "g0", "xl0", "d3", "d1", "g1", "f3", "e0", "e2", "xe1",
+    "t1", "g2", "xe0", "t0", "opt1", "t2", "g3", "opt2", "opt0", "i1", "i0", "i2", "i3", "t3",
 )
 
 
@@ -80,13 +80,15 @@
     x_hbm, gate_hbm, up_hbm, hid_hbm, seg_hbm, dw_hbm, w_hbm, ma_hbm, mo_hbm, se_hbm,
     ig_o, ug_o, gs_o, xt_o, gb, ma_o, mo_o, se_o,
     xs_v, xc_v, xg, gate_v, up_v, hid_v, seg_ref, dw_ref, w_v, xs32, xc32, xq, xp, tw_ref, gp, g32, gr, upo,
-    part, rs_1, rs_2, cnt, cntr, dsum, lsem, wsem, tsem, ssem, rsem,
+    part, rs_1, rs_2, cnt, cntr, dsum, lsem, wsem, tsem, ssem, rsem, both_sem, near_sem, far_sem,
 ):
     r, s = lax.axis_index("replica"), lax.axis_index("shard")
     replicas = lax.axis_size("replica")
     core, side, across = flip(r, 1), flip(r, 2), flip(flip(r, 1), 2)
     near, mid, far = flip(s, 1), flip(s, 2), flip(s, 4)
     mid_far = flip(mid, 4)
+    odd_core = lax.rem(r, 2)
+    inner = lax.rem(lax.rem(lax.div(s, 2), 2) + lax.div(s, 4), 2)
     rows, width = gate_v.shape[0], xc_v.shape[1]
     quarter, tall = rows // QUARTERS, rows // 8
     chunk, span = gb.shape[2], part.shape[2]
@@ -105,11 +107,18 @@
         return copy
 
     barrier = pltpu.get_barrier_semaphore()
-    peers = [(core, s), (side, s), (across, s), (r, near), (r, mid), (r, far)]
-    if "x" in KINDS:
-        peers.append((r, mid_far))
+    peers = [(core, s), (side, s), (across, s)]
     for peer in peers:
         pl.semaphore_signal(barrier, inc=1, device_id=peer, device_id_type=MESH)
+
+    @pl.when(odd_core == 1)
+    def greet_neighbours():
+        for peer in ((r, near), (r, mid)):
+            pl.semaphore_signal(barrier, inc=1, device_id=peer, device_id_type=MESH)
+
+    @pl.when(odd_core * inner == 1)
+    def greet_inner():
+        pl.semaphore_signal(barrier, inc=1, device_id=(r, mid_far), device_id_type=MESH)
 
     l_seg = load(seg_hbm, seg_ref, lsem.at[0])
     l_dw = load(dw_hbm, dw_ref, lsem.at[1])
@@ -150,9 +159,18 @@
     xs32[0] = xs_v[0].astype(f32)
     l_xa.wait()
     xs32[1] = xs_v[1].astype(f32)
-    pl.semaphore_wait(barrier, len(peers))
+    pl.semaphore_wait(barrier, len(peers) + odd_core * (2 + inner))
     counts = [push(cnt, cntr.at[n], (peer, s)) for n, peer in enumerate((core, side, across))]
     x_first = [push(xs32.at[0], xq.at[0, 0], (side, s)), push(xs32.at[1], xq.at[1, 0], (across, s))]
+
+    @pl.when(odd_core == 1)
+    def tell_both_in():
+        for peer in ((r, near), (r, mid)):
+            pl.semaphore_signal(both_sem, inc=1, device_id=peer, device_id_type=MESH)
+
+    @pl.when(odd_core * inner == 1)
+    def tell_both_in_inner():
+        pl.semaphore_signal(both_sem, inc=1, device_id=(r, mid_far), device_id_type=MESH)
 
     for copy in (l_gate, l_hid, l_up):
         copy.wait()
@@ -200,6 +218,8 @@
         part[c] = lax.dot_general(
             gp[...], w_v[pl.ds(c * span, span), :], (((1,), (1,)), ((), ())), preferred_element_type=f32
         )
+        if not first:
+            open_near()
         send_first(c, 0)
 
     def fetch(k):
@@ -219,24 +239,42 @@
         kept = block(c, bit + 4 * (1 - n))
         first[c, n].wait_recv()
         kept[...] = kept[...] + rs_1[c, n]
-        if KINDS[c] == "x" and n == 0:
-            peer = (r, mid_far)
         second[c, n] = push(kept, rs_2.at[c, n], peer)
+
+    def open_near():
+        @pl.when(odd_core == 0)
+        def hear():
+            pl.semaphore_wait(near_sem, 1)
+
+    def pass_near():
+        @pl.when(odd_core == 1)
+        def hear():
+            pl.semaphore_wait(both_sem, 2 + inner)
+            pl.semaphore_signal(near_sem, inc=1, device_id=(core, s), device_id_type=MESH)
+
+        @pl.when(odd_core * inner == 1)
+        def tell():
+            for peer in ((r, mid), (r, mid_far)):
+                pl.semaphore_signal(far_sem, inc=1, device_id=peer, device_id_type=MESH)
+
+    def open_far():
+        pl.semaphore_wait(far_sem, 1)
+
+        @pl.when(odd_core == 1)
+        def tell():
+            pl.semaphore_signal(far_sem, inc=1, device_id=(core, s), device_id_type=MESH)
 
     def forward_far(c):
         kept = block(c, 4)
         first[c, 2].wait_recv()
-        value = kept[...] + rs_1[c, 2]
-        if KINDS[c] != "x":
-            second[c, 0].wait_recv()
-            value = value + rs_2[c, 0]
-        kept[...] = value
+        second[c, 0].wait_recv()
+        kept[...] = kept[...] + rs_1[c, 2] + rs_2[c, 0]
         second[c, 2] = push(kept, rs_2.at[c, 2], (r, far))
 
     def finish(c):
         first[c, 3].wait_recv()
         total = block(c, 0)[...] + rs_1[c, 3]
-        for n in (0, 1, 2) if KINDS[c] == "x" else (1, 2):
+        for n in (1, 2):
             second[c, n].wait_recv()
             total = total + rs_2[c, n]
         ig_o[:, pl.ds(c * span, span)] = (total * scale[0]).astype(bf16)
@@ -319,7 +357,7 @@
     x_core, x_near, x_mid, x_last, g_across, scale = [], {}, {}, {}, {}, []
     steps = {
         "xc": step_xc, "own": step_own, "core": step_core, "scale": step_scale, "x": step_x, "xl": step_x_last,
-        "xe": step_x_end, "st": fetch, "p": project,
+        "xe": step_x_end, "st": fetch, "p": project, "pass": pass_near, "far": open_far,
         "b": lambda c: send_first(c, 1), "c": lambda c: send_first(c, 2), "d": lambda c: send_first(c, 3),
         "a": lambda c: forward(c, 0), "e": lambda c: forward(c, 1), "f": forward_far, "i": finish, "g": relay, "t": take, "opt": optimize,
     }
@@ -401,6 +439,9 @@
             pltpu.SemaphoreType.DMA((3 * CHUNKS,)),
             pltpu.SemaphoreType.DMA((copies,)),
             pltpu.SemaphoreType.DMA((copies,)),
+            pltpu.SemaphoreType.REGULAR,
+            pltpu.SemaphoreType.REGULAR,
+            pltpu.SemaphoreType.REGULAR,
         ],
         compiler_params=pltpu.CompilerParams(
             collective_id=0, has_side_effects=True, vmem_limit_bytes=40 * 1024 * 1024

time: 26.7 us -> 26.3 us (0.985)
  Pallas kernels: 25.9 us -> 25.5 us
    pallas_call x1, Pallas kernels: 23 us -> 22.6 us  [exchange(): pl.pallas_call(exchange_kernel, out_shape=(pltpu.VMEM((tall, features), b...]
where the time goes in v4:
time: 26.3 us; the launch traced here: 26.2 us
  Pallas kernels  25.5 us (97%)
  between operations  0.64 us (2%)
    pallas_call x1, Pallas kernels, exchange(): pl.pallas_call(exchange_kernel, out_shape=(pltpu.VMEM((tall, features), b...  22.6 us
    pallas_call x1, Pallas kernels, step(): pl.pallas_call(step_kernel, out_shape=(jax.ShapeDtypeStruct(ig.shape, ig....  2.9 us

profile of v4, /device:TPU:0, one launch (start us, length us, event | category | flops | bytes accessed | tf_op | source)
XLA Modules:
  0.0 26.2 jit_solution(14311433977546834049)
XLA Ops:
  0.6 22.6 %exchange.1 = (bf16[16,2048]{1,0:T(8,128)(2,1)S(1)}, bf16[128,1024]{1,0:T(8,128)(2,1)S(1)}, f32[8,256]{1,0:T(8,128)S(1)}, bf16[512,512]{1,0:T(8,128)(2,1)S(1)}, ...) custom-call(bf16[128,2048]{1,0:T(8,128)(2,1)} %x_hbm.1, ...), custom_call_target="tpu_custom_call" | custom-call | flops 1073741824 | bytes 12582912 | tf_op jit(solution)/shard_map/exchange/pallas_call | solution.py:398
  23.3 2.9 %step.1 = (bf16[16,2048]{1,0:T(8,128)(2,1)}, bf16[128,1024]{1,0:T(8,128)(2,1)}, f32[512,1024]{1,0:T(8,128)}, f32[512,1024]{1,0:T(8,128)}, f32[512,1024]{1,0:T(8,128)}) custom-call(bf16[16,2048]{1,0:T(8,128)(2,1)S(1)} %get-tuple-element.13.ig_ref, bf16[128,1024]{1,0:T(8,128)(2,1)S(1)} %get-tuple-element.14.ug_ref, f32[8,256]{1,0:T(8,128)S(1)} %get-tuple-element.15.gs_ref, ...), custom_call_target="tpu_custom_call" | custom-call | tf_op jit(solution)/shard_map/step/pallas_call | solution.py:497
